TPU v7x, 32 devices: a whole 2x2x4 slice. The times are simulated.
32 devices in a mesh: out: 8 (over z, y), inp: 4 (over x, core).
Axes of the slice: x: 2, y: 2, z: 4, core: 2. Of those that a mesh axis runs over, the one named last changes fastest.
Arguments:
- weight: float32 [8, 512, 13824], P(None, 'out', 'inp'), may hold values from -6 to 6
- gradient: bfloat16 [8, 512, 13824], P(None, 'out', 'inp'), may hold values from -60 to 60
- momentum: bfloat16 [8, 512, 13824], P(None, 'out', 'inp'), may hold values from -6 to 6
Outputs:
- weight_next: float32 [8, 512, 13824], P(None, 'out', 'inp')
- momentum_next: bfloat16 [8, 512, 13824], P(None, 'out', 'inp')
All inputs are finite; a program needn't handle non-finite values.
Results may differ from a plain program's by a relative error of at most 0.0039.
Values may be sent and summed in bfloat16 or wider, within the bound.
No kernel may reach another device: no remote copies, remote signals or barrier semaphores. Data moves between devices by JAX's collectives and lax.ppermute only.
A program may use at most 64 MiB of HBM per device.

v0:
```python
import math
import jax
import jax.numpy as jnp
from jax import lax
from jax.sharding import PartitionSpec as P

ITERS = 5
COLS = 13824
BETA = 0.95
EPSILON = 1e-06
COEF_A = 3.4445
COEF_B = -4.775
COEF_C = 2.0315


def mult(former, latter):
    return jnp.einsum("kij,kjl->kil", former, latter, precision=lax.Precision.HIGHEST)


def on_device(weight, gradient, momentum):
    moment = BETA * momentum.astype(jnp.float32) + gradient.astype(jnp.float32)
    source = (gradient.astype(jnp.float32) + BETA * moment).astype(jnp.bfloat16)
    local_squares = jnp.einsum("kic,kic->k", source, source, preferred_element_type=jnp.float32)
    totals = lax.psum(local_squares, ("out", "inp")) + EPSILON
    regrouped = lax.all_to_all(source, "out", split_axis=0, concat_axis=1, tiled=True)
    held = regrouped.shape[0]
    width = regrouped.shape[1]
    partial_value = jnp.einsum(
        "kic,kjc->kij", regrouped, regrouped, preferred_element_type=jnp.float32
    )
    scale2 = lax.dynamic_slice_in_dim(totals, lax.axis_index("out") * held, held, 0)
    gram = lax.psum(partial_value.astype(jnp.bfloat16), "inp").astype(jnp.float32)
    current = gram / scale2[:, None, None]
    transform = jnp.broadcast_to(jnp.eye(width, dtype=jnp.float32), (held, width, width))
    for sweep in range(ITERS):
        poly_part = COEF_B * current + COEF_C * mult(current, current)
        transform = COEF_A * transform + mult(poly_part, transform)
        halfway = COEF_A * current + mult(poly_part, current)
        current = COEF_A * halfway + mult(halfway, poly_part)
    factor = (transform / jnp.sqrt(scale2)[:, None, None]).astype(jnp.bfloat16)
    orthogonal = jnp.einsum("kij,kjc->kic", factor, regrouped, preferred_element_type=jnp.float32)
    update = (0.2 * math.sqrt(COLS) * orthogonal).astype(jnp.bfloat16)
    returned = lax.all_to_all(update, "out", split_axis=1, concat_axis=0, tiled=True)
    weight_next = 0.9 * weight - 0.5 * returned.astype(jnp.float32)
    return (weight_next, moment.astype(jnp.bfloat16))


def solution(mesh):
    return jax.shard_map(
        on_device,
        mesh=mesh,
        in_specs=(P(None, "out", "inp"), P(None, "out", "inp"), P(None, "out", "inp")),
        out_specs=(P(None, "out", "inp"), P(None, "out", "inp")),
        check_vma=False,
    )
```

profile of v0, /device:TPU:0, one launch (start us, length us, event | category | flops | bytes accessed | tf_op | source)
XLA Modules:
  0.0 335.9 jit_solution(17814851323513137917)
XLA Ops:
  7.2 0.0 all-reduce.2.cloned.1.call-start
  7.2 4.2 %fusion.1 = (f32[8]{0:T(128)S(1)}, bf16[8,64,3456]{2,1,0:T(8,128)(2,1)S(1)}) fusion(bf16[8,64,3456]{2,1,0:T(8,128)(2,1)} %param.5, bf16[8,64,3456]{2,1,0:T(8,128)(2,1)} %param.4), kind=kLoop, calls=%fused_computation.4 | loop fusion | flops 17694712 | bytes 10616864 | tf_op jit(solution)/shard_map/kic,kic->k/dot_general | solution.py:23
  11.4 86.6 %all_to_all.8 = bf16[8,64,3456]{2,1,0:T(8,128)(2,1)S(1)} all-to-all(bf16[8,64,3456]{2,1,0:T(8,128)(2,1)S(1)} %get-tuple-element.3), channel_id=1, replica_groups=mesh['out'=8,'inp'=4] {'out'}, dimensions={0} | all-to-all | bytes 7077888 | tf_op jit(solution)/shard_map/all_to_all | solution.py:25
  98.0 2.9 fusion.29
  100.9 0.0 all-reduce.2.cloned.1.call-update
  100.9 39.2 %psum.15 = f32[8]{0:T(128)S(1)} all-reduce(f32[8]{0:T(128)S(1)} %get-tuple-element.2), channel_id=1, replica_groups=mesh['out'=8,'inp'=4] {'out','inp'}, use_global_device_ids=true, to_apply=%region_1.0 | all-reduce | flops 8 | bytes 64 | tf_op jit(solution)/shard_map/psum | solution.py:24
  140.1 0.6 dynamic_slice.3
  141.4 0.0 all-reduce.2.cloned.1.call-done
  141.4 0.0 copy-start
  141.4 4.1 %fusion.11 = f32[512,512]{1,0:T(8,128)S(1)} fusion(bf16[1,512,512]{2,1,0:T(8,128)(2,1)} %all-reduce.2.cloned.1.call-done, f32[]{:T(128)} %bitcast.4), kind=kOutput, calls=%fused_computation.35 | convolution fusion | flops 1612447744 | bytes 1572868 | tf_op jit(solution)/shard_map/kij,kjl->kil/dot_general | solution.py:17
  145.5 1.0 convolution_add_fusion.4
  146.5 0.0 copy-done
  146.5 2.6 fusion.12
  149.1 1.8 fusion.13
  150.9 1.9 fusion.15
  152.8 1.8 fusion.16
  154.7 1.8 fusion.17
  156.5 2.1 fusion.19
  158.6 1.8 convolution_add_fusion.3
  160.5 1.8 fusion.20
  162.3 1.8 convolution_add_fusion.2
  164.2 1.8 fusion.21
  166.1 1.9 fusion.23
  167.9 1.8 fusion.24
  169.8 2.1 convolution_add_fusion.1
  171.9 1.8 fusion.25
  173.7 1.9 fusion.27
  175.6 1.9 fusion.28
  177.5 2.1 fusion.3
  179.7 19.5 %copy.14 = bf16[1,512,3456]{2,0,1:T(2,128)(2,1)} copy(bf16[1,512,3456]{2,1,0:T(8,128)(2,1)S(1)} %fusion.3) | data formatting | bytes 7077888 | tf_op jit(solution)/shard_map/convert_element_type | solution.py:42
  199.1 0.5 broadcast.71
  199.7 22.1 %reduce.2 = bf16[512,3456]{1,0:T(8,128)(2,1)S(1)} reduce(bf16[512,1,3456]{2,1,0:T(2,128)(2,1)} %bitcast.144, bf16[]{:T(256)} %broadcast.71), dimensions={1}, to_apply=%bitcast.143.reduce_sub_computation | reduce | bytes 7077890
  221.8 3.7 %reshape.156 = bf16[8,2,110592]{2,1,0:T(2,128)(2,1)} reshape(bf16[512,3456]{1,0:T(8,128)(2,1)S(1)} %reduce.2) | data formatting | bytes 7077888
  225.5 4.9 %all-to-all-start.1 = ((bf16[8,2,110592]{2,1,0:T(2,128)(2,1)}), bf16[8,2,110592]{2,1,0:T(2,128)(2,1)S(1)}, u32[]{:S(2)}, u32[]{:S(2)}) async-start(bf16[8,2,110592]{2,1,0:T(2,128)(2,1)} %reshape.156), calls=%async_computation.1 | async-start | bytes 7077888 | tf_op jit(solution)/shard_map/all_to_all | solution.py:43
  230.5 5.9 %fusion.2 = bf16[8,64,3456]{2,1,0:T(8,128)(2,1)} fusion(bf16[8,64,3456]{2,1,0:T(8,128)(2,1)} %param.4, bf16[8,64,3456]{2,1,0:T(8,128)(2,1)} %param.5), kind=kLoop, calls=%fused_computation.7 | loop fusion | flops 8847360 | bytes 10616832 | tf_op jit(solution)/shard_map/convert_element_type | solution.py:45
  236.4 72.2 %all-to-all-done.1 = bf16[8,2,110592]{2,1,0:T(2,128)(2,1)S(1)} async-done(((bf16[8,2,110592]{2,1,0:T(2,128)(2,1)}), bf16[8,2,110592]{2,1,0:T(2,128)(2,1)S(1)}, u32[]{:S(2)}, u32[]{:S(2)}) %all-to-all-start.1) | async-done | bytes 3538976 | tf_op jit(solution)/shard_map/all_to_all | solution.py:43
  308.6 5.5 %reshape.157 = bf16[512,1,3456]{2,1,0:T(2,128)(2,1)} reshape(bf16[8,2,110592]{2,1,0:T(2,128)(2,1)S(1)} %all-to-all-done.1) | data formatting | bytes 7077888
  314.1 0.0 slice-start
  314.1 9.0 %convert_multiply_fusion.1 = f32[1,512,3456]{2,0,1:T(1,128)S(1)} fusion(bf16[512,1,3456]{2,1,0:T(2,128)(2,1)} %reshape.157), kind=kLoop, calls=%fused_computation.5 | loop fusion | flops 3538944 | bytes 10616832 | tf_op jit(solution)/shard_map/mul | solution.py:44
  323.1 0.0 slice-start.1
  323.2 0.5 copy.12
  323.6 0.0 slice-done
  323.6 1.3 slice-done.1
  325.0 3.9 %multiply_subtract_fusion = f32[8,64,3456]{2,1,0:T(8,128)} fusion(f32[8,64,3456]{2,1,0:T(8,128)S(1)} %bitcast.145, f32[8,64,3456]{2,1,0:T(8,128)S(1)} %bitcast.147), kind=kLoop, calls=%fused_computation.8 | loop fusion | flops 3538944 | bytes 21233664 | tf_op jit(solution)/shard_map/sub | solution.py:44
  (2 shorter events, 0.0 us)
Async XLA Ops:
  7.2 134.3 %all-reduce.2.cloned.1.call-start = ((), (), s32[]{:S(2)}) async-start(), calls=%async_computation.2 | async-start | bytes 1048576 | tf_op jit(solution)/shard_map/psum | solution.py:32
  141.4 5.1 %copy-start = (bf16[1,512,512]{2,1,0:T(8,128)(2,1)S(1)}, bf16[1,512,512]{2,1,0:T(8,128)(2,1)}, u32[]{:S(2)}) copy-start(bf16[1,512,512]{2,1,0:T(8,128)(2,1)} %all-reduce.2.cloned.1.call-done) | copy-start | bytes 1572868
  225.5 83.0 %all-to-all-start.1 = ((bf16[8,2,110592]{2,1,0:T(2,128)(2,1)}), bf16[8,2,110592]{2,1,0:T(2,128)(2,1)S(1)}, u32[]{:S(2)}, u32[]{:S(2)}) async-start(bf16[8,2,110592]{2,1,0:T(2,128)(2,1)} %reshape.156), calls=%async_computation.1 | async-start | bytes 7077888 | tf_op jit(solution)/shard_map/all_to_all | solution.py:43
  314.1 9.5 %slice-start = ((s8[7077888]{0:T(1024)(128)(4,1)}), s8[4194304]{0:T(1024)(128)(4,1)S(1)}, s32[]{:S(2)}) async-start(s8[7077888]{0:T(1024)(128)(4,1)} %bitcast.146), calls=%async_computation.3 | async-start | bytes 8388608
  323.1 1.8 slice-start.1
Sparse Core Ops, SparseCore 0:
  101.0 32.2 all-reduce.1
where the time goes:
time: 339 us; the launch traced here: 336 us
  blocking collectives  126 us (37%)
  waiting for transfers between devices  72.2 us (21%)
  other arithmetic  45.2 us (13%)
  matrix products  40.9 us (12%)
  local copies, waits for them, and re-layouts  31.6 us (9%)
  between operations  15.2 us (4%)
  starting transfers between devices  4.98 us (1%)
    all_to_all x1, blocking collectives, on_device(): lax.all_to_all(source, 'out', split_axis=0, concat_axis=1, tiled=True)  86.6 us
    all_to_all x1, waiting for transfers between devices, on_device(): lax.all_to_all(update, 'out', split_axis=1, concat_axis=0, tiled=True)  72.2 us
    psum x1, blocking collectives, on_device(): totals = lax.psum(local_squares, ('out', 'inp')) + EPSILON  39.2 us
    dot_general x18, matrix products, mult(): jnp.einsum('kij,kjl->kil', former, latter, precision=lax.Precision.HIGHEST)  36 us
    unnamed x2, other arithmetic  22.1 us
    convert_element_type x1, local copies, waits for them, and re-layouts, on_device(): update = (0.2 * math.sqrt(COLS) * orthogonal).astype(jnp.bfloat16)  19.5 us
    unnamed x10, local copies, waits for them, and re-layouts  11.6 us
    mul x1, other arithmetic, on_device(): weight_next = 0.9 * weight - 0.5 * returned.astype(jnp.float32)  9.03 us
  transfers between devices with their start and end apart: 2, of which 1 were waited for; matrix products, arithmetic and copies ran while one was open for 2% of the time, Pallas kernels for 0%

commit v1 on v0

--- a/solution.py
+++ b/solution.py
@@ -1,3 +1,4 @@
+import functools
 import math
 import jax
 import jax.numpy as jnp
@@ -11,6 +12,33 @@
 COEF_A = 3.4445
 COEF_B = -4.775
 COEF_C = 2.0315
+
+
+def open_frame(xx, dim_k, x0):
+    big, after = (xx.shape[:dim_k], xx.shape[dim_k + 1 :])
+    return jnp.moveaxis(xx.reshape(*big, x0, -1, *after), dim_k, 0)
+
+
+def draw_stocks(w_in, join_dim):
+    w_in = jnp.moveaxis(w_in, 0, join_dim)
+    back = w_in.shape
+    return w_in.reshape(
+        *back[:join_dim], back[join_dim] * back[join_dim + 1], *back[join_dim + 2 :]
+    )
+
+
+def refer_steps_all_by_axis(a0, mesh_ax, x_local, raw):
+    oldest, row_out = (lax.axis_size(mesh_ax), lax.axis_index(mesh_ax))
+    current_arr = open_frame(a0, x_local, oldest)
+    entries = [current_arr[row_out]]
+    for w in tuple(range(1, oldest)):
+        w2 = current_arr[row_out ^ w]
+        entries.append(lax.ppermute(w2, mesh_ax, [(m, m ^ w) for m in range(oldest)]))
+    current_arr = jnp.stack(entries, axis=0)[row_out ^ jnp.arange(oldest)]
+    return draw_stocks(current_arr, raw)
+
+
+set_windows = functools.partial(refer_steps_all_by_axis, mesh_ax="out", x_local=1, raw=0)
 
 
 def mult(former, latter):
@@ -40,7 +68,7 @@
     factor = (transform / jnp.sqrt(scale2)[:, None, None]).astype(jnp.bfloat16)
     orthogonal = jnp.einsum("kij,kjc->kic", factor, regrouped, preferred_element_type=jnp.float32)
     update = (0.2 * math.sqrt(COLS) * orthogonal).astype(jnp.bfloat16)
-    returned = lax.all_to_all(update, "out", split_axis=1, concat_axis=0, tiled=True)
+    returned = set_windows(update)
     weight_next = 0.9 * weight - 0.5 * returned.astype(jnp.float32)
     return (weight_next, moment.astype(jnp.bfloat16))
 

time: 339 us -> 287 us (0.85)
  the two profiles are of different devices: /device:TPU:0 before, /device:TPU:10 now
where the time goes in v1:
time: 287 us; the launch traced here: 284 us
  blocking collectives  125 us (44%)
  waiting for transfers between devices  70.8 us (25%)
  matrix products  41.3 us (14%)
  between operations  15.3 us (5%)
  other arithmetic  14 us (5%)
  starting transfers between devices  9.7 us (3%)
  local copies, waits for them, and re-layouts  7.72 us (3%)
    all_to_all x1, blocking collectives, on_device(): lax.all_to_all(source, 'out', split_axis=0, concat_axis=1, tiled=True)  84.4 us
    ppermute x7, waiting for transfers between devices, refer_steps_all_by_axis(): lax.ppermute(w2, mesh_ax, [(m, m ^ w) for m in range(oldest)])  70.8 us
    psum x1, blocking collectives, on_device(): totals = lax.psum(local_squares, ('out', 'inp')) + EPSILON  40.6 us
    dot_general x18, matrix products, mult(): jnp.einsum('kij,kjl->kil', former, latter, precision=lax.Precision.HIGHEST)  36.3 us
    ppermute x7, starting transfers between devices, refer_steps_all_by_axis(): lax.ppermute(w2, mesh_ax, [(m, m ^ w) for m in range(oldest)])  9.66 us
    sub x1, other arithmetic, on_device(): weight_next = 0.9 * weight - 0.5 * returned.astype(jnp.float32)  6.9 us
  transfers between devices with their start and end apart: 8, of which 5 were waited for; matrix products, arithmetic and copies ran while one was open for 1% of the time, Pallas kernels for 0%

profile of v1, /device:TPU:10, one launch (start us, length us, event | category | flops | bytes accessed | tf_op | source)
XLA Modules:
  0.0 283.9 jit_solution(2307529159286097660)
XLA Ops:
  7.2 0.0 all-reduce.2.cloned.1.call-start
  7.2 4.2 %fusion.1 = (f32[8]{0:T(128)S(1)}, bf16[8,64,3456]{2,1,0:T(8,128)(2,1)S(1)}) fusion(bf16[8,64,3456]{2,1,0:T(8,128)(2,1)} %param.5, bf16[8,64,3456]{2,1,0:T(8,128)(2,1)} %param.4), kind=kLoop, calls=%fused_computation.5 | loop fusion | flops 17694712 | bytes 10616864 | tf_op jit(solution)/shard_map/kic,kic->k/dot_general | solution.py:51
  11.4 84.4 %all_to_all.4 = bf16[8,64,3456]{2,1,0:T(8,128)(2,1)S(1)} all-to-all(bf16[8,64,3456]{2,1,0:T(8,128)(2,1)S(1)} %get-tuple-element.3), channel_id=1, replica_groups=mesh['out'=8,'inp'=4] {'out'}, dimensions={0} | all-to-all | bytes 7077888 | tf_op jit(solution)/shard_map/all_to_all | solution.py:53
  95.9 2.9 %fusion.28 = bf16[1,512,512]{2,1,0:T(8,128)(2,1)} fusion(bf16[512,3456]{1,0:T(8,128)(2,1)S(1)} %bitcast.169), kind=kOutput, calls=%fused_computation.53 | convolution fusion | flops 1812201472 | bytes 4063232 | tf_op jit(solution)/shard_map/kic,kjc->kij/dot_general | solution.py:56
  98.8 0.0 all-reduce.2.cloned.1.call-update
  98.8 40.6 %psum.15 = f32[8]{0:T(128)S(1)} all-reduce(f32[8]{0:T(128)S(1)} %get-tuple-element.2), channel_id=1, replica_groups=mesh['out'=8,'inp'=4] {'out','inp'}, use_global_device_ids=true, to_apply=%region_1.0 | all-reduce | flops 8 | bytes 64 | tf_op jit(solution)/shard_map/psum | solution.py:52
  139.5 0.6 dynamic_slice.27
  140.8 0.0 all-reduce.2.cloned.1.call-done
  140.8 0.0 copy-start.3
  140.8 4.2 %fusion.10 = f32[512,512]{1,0:T(8,128)S(1)} fusion(bf16[1,512,512]{2,1,0:T(8,128)(2,1)} %all-reduce.2.cloned.1.call-done, f32[]{:T(128)} %bitcast.4), kind=kOutput, calls=%fused_computation.34 | convolution fusion | flops 1612447744 | bytes 1572868 | tf_op jit(solution)/shard_map/kij,kjl->kil/dot_general | solution.py:45
  145.0 1.0 convolution_add_fusion.4
  146.0 0.0 copy-done.3
  146.0 2.6 fusion.11
  148.6 1.8 fusion.12
  150.5 1.9 fusion.14
  152.3 1.8 fusion.15
  154.2 1.8 convolution_add_fusion.3
  156.1 2.0 fusion.16
  158.1 1.9 fusion.18
  160.0 1.8 fusion.19
  161.8 1.9 convolution_add_fusion.2
  163.7 1.8 fusion.20
  165.6 1.9 fusion.22
  167.5 1.9 fusion.23
  169.4 2.1 convolution_add_fusion.1
  171.5 1.9 fusion.24
  173.4 1.9 fusion.26
  175.3 1.9 fusion.27
  177.2 2.1 multiply_convert_fusion
  179.4 0.0 copy-start
  179.4 0.0 copy-start.1
  179.4 0.3 dynamic-slice_bitcast_fusion
  179.7 1.0 collective-permute-start
  180.7 0.7 copy-done
  181.4 1.1 copy-done.1
  182.5 2.9 %fusion.2 = bf16[8,64,3456]{2,1,0:T(8,128)(2,1)} fusion(bf16[8,64,3456]{2,1,0:T(8,128)(2,1)S(1)} %copy-done.1, bf16[8,64,3456]{2,1,0:T(8,128)(2,1)S(1)} %copy-done), kind=kLoop, calls=%fused_computation.8 | loop fusion | flops 8847360 | bytes 10616832 | tf_op jit(solution)/shard_map/convert_element_type | solution.py:73
  185.4 0.5 collective-permute-start.1
  185.8 2.0 collective-permute-start.2
  187.8 1.0 collective-permute-start.3
  188.8 2.5 collective-permute-start.4
  191.3 0.0 collective-permute-done
  191.3 0.6 collective-permute-start.5
  191.9 20.9 %collective-permute-done.1 = bf16[1,64,3456]{2,1,0:T(8,128)(2,1)S(1)} collective-permute-done((bf16[1,64,3456]{2,1,0:T(8,128)(2,1)S(1)}, bf16[1,64,3456]{2,1,0:T(8,128)(2,1)S(1)}, u32[]{:S(2)}, u32[]{:S(2)}) %collective-permute-start.1) | collective-permute-done | bytes 442400 | tf_op jit(solution)/shard_map/ppermute | solution.py:36
  212.8 2.1 collective-permute-start.6
  215.0 5.3 %collective-permute-done.2 = bf16[1,64,3456]{2,1,0:T(8,128)(2,1)S(1)} collective-permute-done((bf16[1,64,3456]{2,1,0:T(8,128)(2,1)S(1)}, bf16[1,64,3456]{2,1,0:T(8,128)(2,1)S(1)}, u32[]{:S(2)}, u32[]{:S(2)}) %collective-permute-start.2) | collective-permute-done | bytes 442400 | tf_op jit(solution)/shard_map/ppermute | solution.py:36
  220.4 0.0 collective-permute-done.3
  220.4 26.3 %collective-permute-done.4 = bf16[1,64,3456]{2,1,0:T(8,128)(2,1)S(1)} collective-permute-done((bf16[1,64,3456]{2,1,0:T(8,128)(2,1)S(1)}, bf16[1,64,3456]{2,1,0:T(8,128)(2,1)S(1)}, u32[]{:S(2)}, u32[]{:S(2)}) %collective-permute-start.4) | collective-permute-done | bytes 442400 | tf_op jit(solution)/shard_map/ppermute | solution.py:36
  246.8 11.3 %collective-permute-done.5 = bf16[1,64,3456]{2,1,0:T(8,128)(2,1)S(1)} collective-permute-done((bf16[1,64,3456]{2,1,0:T(8,128)(2,1)S(1)}, bf16[1,64,3456]{2,1,0:T(8,128)(2,1)S(1)}, u32[]{:S(2)}, u32[]{:S(2)}) %collective-permute-start.5) | collective-permute-done | bytes 442400 | tf_op jit(solution)/shard_map/ppermute | solution.py:36
  258.1 7.0 %collective-permute-done.6 = bf16[1,64,3456]{2,1,0:T(8,128)(2,1)S(1)} collective-permute-done((bf16[1,64,3456]{2,1,0:T(8,128)(2,1)S(1)}, bf16[1,64,3456]{2,1,0:T(8,128)(2,1)S(1)}, u32[]{:S(2)}, u32[]{:S(2)}) %collective-permute-start.6) | collective-permute-done | bytes 442400 | tf_op jit(solution)/shard_map/ppermute | solution.py:36
  265.1 0.0 copy-start.2
  265.1 1.8 copy-done.2
  266.9 3.0 %gather_fusion = bf16[8,64,3456]{2,1,0:T(8,128)(2,1)S(1)} fusion(bf16[8,64,3456]{2,1,0:T(8,128)(2,1)} %bitcast.168, s32[1024]{0:T(1024)S(1)} %pad_clamp_fusion), kind=kCustom, calls=%fused_computation | custom fusion | bytes 7077920 | tf_op jit(solution)/shard_map/gather | solution.py:37
  270.0 6.9 %multiply_subtract_fusion = f32[8,64,3456]{2,1,0:T(8,128)} fusion(bf16[8,64,3456]{2,1,0:T(8,128)(2,1)S(1)} %gather_fusion, f32[8,64,3456]{2,1,0:T(8,128)} %param.3), kind=kLoop, calls=%fused_computation.6 | loop fusion | flops 7077888 | bytes 17694720 | tf_op jit(solution)/shard_map/sub | solution.py:72
  (10 shorter events, 0.3 us)
Async XLA Ops:
  7.2 133.6 %all-reduce.2.cloned.1.call-start = ((), (), s32[]{:S(2)}) async-start(), calls=%async_computation.1 | async-start | bytes 1048576 | tf_op jit(solution)/shard_map/psum | solution.py:60
  140.8 5.2 %copy-start.3 = (bf16[1,512,512]{2,1,0:T(8,128)(2,1)S(1)}, bf16[1,512,512]{2,1,0:T(8,128)(2,1)}, u32[]{:S(2)}) copy-start(bf16[1,512,512]{2,1,0:T(8,128)(2,1)} %all-reduce.2.cloned.1.call-done) | copy-start | bytes 1572868
  179.4 2.0 copy-start
  179.4 3.1 %copy-start.1 = (bf16[8,64,3456]{2,1,0:T(8,128)(2,1)S(1)}, bf16[8,64,3456]{2,1,0:T(8,128)(2,1)}, u32[]{:S(2)}) copy-start(bf16[8,64,3456]{2,1,0:T(8,128)(2,1)} %param.4) | copy-start | bytes 10616836
  179.7 11.6 %collective-permute-start = (bf16[1,64,3456]{2,1,0:T(8,128)(2,1)S(1)}, bf16[1,64,3456]{2,1,0:T(8,128)(2,1)S(1)}, u32[]{:S(2)}, u32[]{:S(2)}) collective-permute-start(bf16[1,64,3456]{2,1,0:T(8,128)(2,1)S(1)} %get-tuple-element.10), channel_id=1, source_target_pairs={{0,4},{4,0},{8,12},{12,8},{16,20},{20,16},{24,28},{28,24},{1,5},{5... | collective-permute-start | bytes 1327112 | tf_op jit(solution)/shard_map/ppermute | solution.py:36
  185.4 27.5 %collective-permute-start.1 = (bf16[1,64,3456]{2,1,0:T(8,128)(2,1)S(1)}, bf16[1,64,3456]{2,1,0:T(8,128)(2,1)S(1)}, u32[]{:S(2)}, u32[]{:S(2)}) collective-permute-start(bf16[1,64,3456]{2,1,0:T(8,128)(2,1)S(1)} %get-tuple-element.9), channel_id=1, source_target_pairs={{0,8},{4,12},{8,0},{12,4},{16,24},{20,28},{24,16},{28,20},{1,9},{5... | collective-permute-start | bytes 1327112 | tf_op jit(solution)/shard_map/ppermute | solution.py:36
  185.8 34.5 %collective-permute-start.2 = (bf16[1,64,3456]{2,1,0:T(8,128)(2,1)S(1)}, bf16[1,64,3456]{2,1,0:T(8,128)(2,1)S(1)}, u32[]{:S(2)}, u32[]{:S(2)}) collective-permute-start(bf16[1,64,3456]{2,1,0:T(8,128)(2,1)S(1)} %get-tuple-element.8), channel_id=1, source_target_pairs={{0,12},{4,8},{8,4},{12,0},{16,28},{20,24},{24,20},{28,16},{1,13},{... | collective-permute-start | bytes 1327112 | tf_op jit(solution)/shard_map/ppermute | solution.py:36
  187.8 32.5 %collective-permute-start.3 = (bf16[1,64,3456]{2,1,0:T(8,128)(2,1)S(1)}, bf16[1,64,3456]{2,1,0:T(8,128)(2,1)S(1)}, u32[]{:S(2)}, u32[]{:S(2)}) collective-permute-start(bf16[1,64,3456]{2,1,0:T(8,128)(2,1)S(1)} %get-tuple-element.7), channel_id=1, source_target_pairs={{0,16},{4,20},{8,24},{12,28},{16,0},{20,4},{24,8},{28,12},{1,17},{... | collective-permute-start | bytes 1327112 | tf_op jit(solution)/shard_map/ppermute | solution.py:36
  188.8 58.0 %collective-permute-start.4 = (bf16[1,64,3456]{2,1,0:T(8,128)(2,1)S(1)}, bf16[1,64,3456]{2,1,0:T(8,128)(2,1)S(1)}, u32[]{:S(2)}, u32[]{:S(2)}) collective-permute-start(bf16[1,64,3456]{2,1,0:T(8,128)(2,1)S(1)} %get-tuple-element.6), channel_id=1, source_target_pairs={{0,20},{4,16},{8,28},{12,24},{16,4},{20,0},{24,12},{28,8},{1,21},{... | collective-permute-start | bytes 1327112 | tf_op jit(solution)/shard_map/ppermute | solution.py:36
  191.3 66.8 %collective-permute-start.5 = (bf16[1,64,3456]{2,1,0:T(8,128)(2,1)S(1)}, bf16[1,64,3456]{2,1,0:T(8,128)(2,1)S(1)}, u32[]{:S(2)}, u32[]{:S(2)}) collective-permute-start(bf16[1,64,3456]{2,1,0:T(8,128)(2,1)S(1)} %get-tuple-element.5), channel_id=1, source_target_pairs={{0,24},{4,28},{8,16},{12,20},{16,8},{20,12},{24,0},{28,4},{1,25},{... | collective-permute-start | bytes 1327112 | tf_op jit(solution)/shard_map/ppermute | solution.py:36
  212.8 52.2 %collective-permute-start.6 = (bf16[1,64,3456]{2,1,0:T(8,128)(2,1)S(1)}, bf16[1,64,3456]{2,1,0:T(8,128)(2,1)S(1)}, u32[]{:S(2)}, u32[]{:S(2)}) collective-permute-start(bf16[1,64,3456]{2,1,0:T(8,128)(2,1)S(1)} %get-tuple-element.4), channel_id=1, source_target_pairs={{0,28},{4,24},{8,20},{12,16},{16,12},{20,8},{24,4},{28,0},{1,29},{... | collective-permute-start | bytes 1327112 | tf_op jit(solution)/shard_map/ppermute | solution.py:36
  265.1 1.8 copy-start.2
Sparse Core Ops, SparseCore 0:
  98.9 31.7 all-reduce.1
